TPU v7x, 32 devices: a whole 2x2x4 slice. The times are simulated.
32 devices in a mesh: dp: 4 (over z), row: 2 (over x), col: 4 (over y, core).
Axes of the slice: x: 2, y: 2, z: 4, core: 2. Of those that a mesh axis runs over, the one named last changes fastest.
Arguments:
- inputs: bfloat16 [4096, 1536], P(('dp', 'row'), 'col'), may hold values from -12.5 to 12.5
- gain_attn: bfloat16 [1536], P(('col', 'dp')), may hold values from 0.25 to 1.75
- w_query: bfloat16 [1536, 1536], P(('col', 'dp'), 'row'), may hold values from -0.15625 to 0.15625
- b_query: bfloat16 [1536], P(('row', 'dp')), may hold values from -3 to 3
- key_weight: bfloat16 [1536, 256], P(('col', 'dp'), 'row'), may hold values from -0.15625 to 0.15625
- key_bias: bfloat16 [256], P(('row', 'dp')), may hold values from -3 to 3
- value_weight: bfloat16 [1536, 256], P(('col', 'dp'), 'row'), may hold values from -0.15625 to 0.15625
- value_bias: bfloat16 [256], P(('row', 'dp')), may hold values from -3 to 3
- w_output: bfloat16 [1536, 1536], P(('row', 'dp'), 'col'), may hold values from -1.25 to 1.25
- gain_mlp: bfloat16 [1536], P(('col', 'dp')), may hold values from 0.25 to 1.75
- w_gate: bfloat16 [1536, 8960], P(('col', 'dp'), 'row'), may hold values from -0.15625 to 0.15625
- w_up: bfloat16 [1536, 8960], P(('col', 'dp'), 'row'), may hold values from -0.15625 to 0.15625
- w_down: bfloat16 [8960, 1536], P(('row', 'dp'), 'col'), may hold values from -0.0625 to 0.0625
- cotangent: bfloat16 [4096, 1536], P(('dp', 'row'), 'col'), may hold values from -6 to 6
Outputs:
- outputs: bfloat16 [4096, 1536], P(('dp', 'row'), 'col')
- grad_inputs: bfloat16 [4096, 1536], P(('dp', 'row'), 'col')
- grad_gain_attn: float32 [1536], P(('col', 'dp'))
- grad_w_query: float32 [1536, 1536], P(('col', 'dp'), 'row')
- grad_b_query: float32 [1536], P(('row', 'dp'))
- grad_w_key: float32 [1536, 256], P(('col', 'dp'), 'row')
- grad_b_key: float32 [256], P(('row', 'dp'))
- grad_w_value: float32 [1536, 256], P(('col', 'dp'), 'row')
- grad_b_value: float32 [256], P(('row', 'dp'))
- grad_w_output: float32 [1536, 1536], P(('row', 'dp'), 'col')
- grad_gain_mlp: float32 [1536], P(('col', 'dp'))
- grad_w_gate: float32 [1536, 8960], P(('col', 'dp'), 'row')
- grad_w_up: float32 [1536, 8960], P(('col', 'dp'), 'row')
- grad_w_down: float32 [8960, 1536], P(('row', 'dp'), 'col')
All inputs are finite; a program needn't handle non-finite values.
Results may differ from a plain program's by a relative error of at most 0.025.
Values may be sent and summed in bfloat16 or wider, within the bound.
A program may use at most 256 MiB of HBM per device.

v0:
```python
import jax
import jax.numpy as jnp
from jax import lax
from jax.sharding import PartitionSpec as P

MODEL_WIDTH = 1536
HEAD_SIZE = 128


epsilon = 1e-06
rope_base = 1000000.0


def shortened(shard):
    return jax.tree.map(lambda a: a.astype(jnp.bfloat16) if a.dtype == jnp.float32 else a, shard)


def rope_turn(value_rows, positions, direction):
    row_count = value_rows.shape[0]
    heads = value_rows.shape[1] // HEAD_SIZE
    half = HEAD_SIZE // 2
    freqs = rope_base ** (-(jnp.arange(half, dtype=jnp.float32) * 2.0 / HEAD_SIZE))
    angles = positions.astype(jnp.float32)[:, None] * freqs[None, :]
    cosine = jnp.cos(angles)[:, None, :]
    sine = direction * jnp.sin(angles)[:, None, :]
    shaped = value_rows.reshape(row_count, heads, HEAD_SIZE)
    first = shaped[..., :half]
    second = shaped[..., half:]
    turned = jnp.concatenate([first * cosine - second * sine, second * cosine + first * sine], -1)
    return turned.reshape(row_count, heads * HEAD_SIZE)


def outer_sum(left, right):
    return lax.dot_general(
        left, right, (((0,), (0,)), ((), ())), preferred_element_type=jnp.float32
    )


def back_product(left, weight):
    return lax.dot_general(
        left, weight, (((1,), (1,)), ((), ())), preferred_element_type=jnp.float32
    )


def norm_forward(value_rows, gain):
    squares = lax.psum(jnp.sum(value_rows * value_rows, axis=1), "col")
    inv_rms = lax.rsqrt(squares / MODEL_WIDTH + epsilon)[:, None]
    return (value_rows * inv_rms * gain.astype(jnp.float32), inv_rms)


def norm_backward(value_rows, inv_rms, gain, grad_in):
    weighted = grad_in * gain.astype(jnp.float32)
    inner = lax.psum(jnp.sum(weighted * value_rows, axis=1), "col")[:, None]
    return inv_rms * weighted - value_rows * inv_rms * inv_rms * inv_rms * inner / MODEL_WIDTH


def rows_whole(local):
    return lax.all_gather(local, "row", axis=0, tiled=True)


def cols_whole(local):
    return jax.tree.map(
        lambda part, own: part.astype(own.dtype),
        lax.all_gather(shortened(local), "col", axis=0, tiled=True),
        local,
    )


def rows_sum(term):
    return lax.psum_scatter(term, "row", scatter_dimension=0, tiled=True)


def width_sum(whole, weight, contract):

    def term(first_row, row_count):
        return lax.dot_general(
            whole, weight, (((1,), (contract,)), ((), ())), preferred_element_type=jnp.float32
        )

    return lax.psum_scatter(
        term(jnp.int32(0), lax.axis_size("col") * (whole.shape[0] // lax.axis_size("col"))),
        "col",
        scatter_dimension=0,
        tiled=True,
    )


def score_block(query_rows, keys_all, positions):
    rows_per_block = query_rows.shape[0]
    kv_heads = keys_all.shape[1] // HEAD_SIZE
    heads_per_group = query_rows.shape[1] // HEAD_SIZE // kv_heads
    query_four = query_rows.reshape(rows_per_block, kv_heads, heads_per_group, HEAD_SIZE)
    keys_triple_shape = keys_all.reshape(keys_all.shape[0], kv_heads, HEAD_SIZE)
    scores = jnp.einsum(
        "ikgd,jkd->kgij", query_four, keys_triple_shape, preferred_element_type=jnp.float32
    ) * HEAD_SIZE ** (-0.5)
    admitted = jnp.arange(keys_all.shape[0], dtype=jnp.int32)[None, :] <= positions[:, None]
    return (jnp.where(admitted, scores, -1e30), query_four, keys_triple_shape)


def attend_forward(query_rows, keys_all, values_all, positions):
    scores, query_four, keys_triple_shape = score_block(query_rows, keys_all, positions)
    top_score = jnp.max(scores, axis=-1, keepdims=True)
    expo = jnp.exp(scores - top_score)
    totals = jnp.sum(expo, axis=-1, keepdims=True)
    probs = (expo / totals).astype(jnp.bfloat16)
    log_total = (top_score + jnp.log(totals))[..., 0]
    values_triple_shape = values_all.reshape(keys_triple_shape.shape)
    attended = jnp.einsum(
        "kgij,jkd->ikgd", probs, values_triple_shape, preferred_element_type=jnp.float32
    )
    return (attended.reshape(query_rows.shape).astype(jnp.bfloat16), log_total)


def attend_backward(query_rows, keys_all, values_all, positions, log_total, d_attended):
    scores, query_four, keys_triple_shape = score_block(query_rows, keys_all, positions)
    probs = jnp.exp(scores - log_total[..., None])
    probs_low = probs.astype(jnp.bfloat16)
    values_triple_shape = values_all.reshape(keys_triple_shape.shape)
    grad_four = d_attended.reshape(query_four.shape)
    d_probs = jnp.einsum(
        "ikgd,jkd->kgij", grad_four, values_triple_shape, preferred_element_type=jnp.float32
    )
    centre = jnp.sum(probs * d_probs, axis=-1, keepdims=True)
    d_scores = (probs * (d_probs - centre)).astype(jnp.bfloat16)
    d_queries = jnp.einsum(
        "kgij,jkd->ikgd", d_scores, keys_triple_shape, preferred_element_type=jnp.float32
    )
    d_keys = jnp.einsum("kgij,ikgd->jkd", d_scores, query_four, preferred_element_type=jnp.float32)
    d_values = jnp.einsum(
        "kgij,ikgd->jkd", probs_low, grad_four, preferred_element_type=jnp.float32
    )
    scale_factor = HEAD_SIZE ** (-0.5)
    return (
        d_queries.reshape(query_rows.shape) * scale_factor,
        d_keys.reshape(keys_all.shape) * scale_factor,
        d_values.reshape(values_all.shape),
    )


def shards(
    inputs,
    gain_attn,
    w_query,
    b_query,
    key_weight,
    key_bias,
    value_weight,
    value_bias,
    w_output,
    gain_mlp,
    w_gate,
    w_up,
    w_down,
    cotangent,
):
    (
        gain_attn,
        w_query,
        b_query,
        key_weight,
        key_bias,
        value_weight,
        value_bias,
        w_output,
        gain_mlp,
        w_gate,
        w_up,
        w_down,
    ) = (
        lax.all_gather(gain_attn, "dp", axis=0, tiled=True),
        lax.all_gather(w_query, "dp", axis=0, tiled=True),
        lax.all_gather(b_query, "dp", axis=0, tiled=True),
        lax.all_gather(key_weight, "dp", axis=0, tiled=True),
        lax.all_gather(key_bias, "dp", axis=0, tiled=True),
        lax.all_gather(value_weight, "dp", axis=0, tiled=True),
        lax.all_gather(value_bias, "dp", axis=0, tiled=True),
        lax.all_gather(w_output, "dp", axis=0, tiled=True),
        lax.all_gather(gain_mlp, "dp", axis=0, tiled=True),
        lax.all_gather(w_gate, "dp", axis=0, tiled=True),
        lax.all_gather(w_up, "dp", axis=0, tiled=True),
        lax.all_gather(w_down, "dp", axis=0, tiled=True),
    )
    local_rows = inputs.shape[0]
    seq_len = local_rows * lax.axis_size("row")
    rows_per_block = seq_len // lax.axis_size("col")
    positions = lax.axis_index("col") * rows_per_block + jnp.arange(rows_per_block, dtype=jnp.int32)
    width_q = w_query.shape[1]
    width_kv = key_weight.shape[1]
    units = w_gate.shape[1]
    inputs_wide = inputs.astype(jnp.float32)
    normed1, inv_rms1 = norm_forward(inputs_wide, gain_attn)
    normed1_all = rows_whole(normed1.astype(jnp.bfloat16))
    projected = width_sum(normed1_all, jnp.concatenate([w_query, key_weight, value_weight], 1), 0)
    projected = projected + jnp.concatenate([b_query, key_bias, value_bias]).astype(jnp.float32)
    query_rows = rope_turn(projected[:, :width_q], positions, 1.0).astype(jnp.bfloat16)
    rotated_keys = rope_turn(projected[:, width_q : width_q + width_kv], positions, 1.0).astype(
        jnp.bfloat16
    )
    value_rows = projected[:, width_q + width_kv :].astype(jnp.bfloat16)
    keys_all, values_all = (
        lax.all_gather(rotated_keys, "col", axis=0, tiled=True),
        lax.all_gather(value_rows, "col", axis=0, tiled=True),
    )
    attended, log_total = attend_forward(query_rows, keys_all, values_all, positions)
    attended_all = cols_whole(attended)
    middle = inputs_wide + rows_sum(
        jnp.dot(attended_all, w_output, preferred_element_type=jnp.float32)
    )
    normed2, inv_rms2 = norm_forward(middle, gain_mlp)
    normed2_all = rows_whole(normed2.astype(jnp.bfloat16))
    both_pre = width_sum(normed2_all, jnp.concatenate([w_gate, w_up], 1), 0)
    gate_pre = both_pre[:, :units]
    up_pre = both_pre[:, units:]
    sigmoid_gate = jax.nn.sigmoid(gate_pre)
    silu_gate = gate_pre * sigmoid_gate
    hidden = (silu_gate * up_pre).astype(jnp.bfloat16)
    hidden_all = cols_whole(hidden)
    outputs = middle + rows_sum(jnp.dot(hidden_all, w_down, preferred_element_type=jnp.float32))
    cot_all = rows_whole(cotangent)
    grad_down = outer_sum(hidden_all, cot_all)
    d_hidden = width_sum(cot_all, w_down, 1)
    d_gate = (d_hidden * up_pre * sigmoid_gate * (1.0 + gate_pre * (1.0 - sigmoid_gate))).astype(
        jnp.bfloat16
    )
    d_up = (d_hidden * silu_gate).astype(jnp.bfloat16)
    d_gate_all, d_up_all = cols_whole((d_gate, d_up))
    grad_gate = outer_sum(normed2_all, d_gate_all)
    grad_up = outer_sum(normed2_all, d_up_all)
    d_norm2 = rows_sum(back_product(d_gate_all, w_gate) + back_product(d_up_all, w_up))
    d_middle = cotangent.astype(jnp.float32) + norm_backward(middle, inv_rms2, gain_mlp, d_norm2)
    d_middle_all = rows_whole(d_middle.astype(jnp.bfloat16))
    grad_output = outer_sum(attended_all, d_middle_all)
    d_attended = width_sum(d_middle_all, w_output, 1).astype(jnp.bfloat16)
    d_queries, d_keys_part, d_values_part = attend_backward(
        query_rows, keys_all, values_all, positions, log_total, d_attended
    )
    d_keys, d_values = (
        lax.psum_scatter(d_keys_part, "col", scatter_dimension=0, tiled=True),
        lax.psum_scatter(d_values_part, "col", scatter_dimension=0, tiled=True),
    )
    d_query_low = rope_turn(d_queries, positions, -1.0).astype(jnp.bfloat16)
    d_key_low = rope_turn(d_keys, positions, -1.0).astype(jnp.bfloat16)
    d_value_low = d_values.astype(jnp.bfloat16)
    d_query_all, d_key_all, d_value_all = cols_whole((d_query_low, d_key_low, d_value_low))
    grad_query = outer_sum(normed1_all, d_query_all)
    grad_key = outer_sum(normed1_all, d_key_all)
    grad_value = outer_sum(normed1_all, d_value_all)
    grad_bias_q = jnp.sum(d_query_all, axis=0, dtype=jnp.float32)
    grad_bias_k = jnp.sum(d_key_all, axis=0, dtype=jnp.float32)
    grad_bias_v = jnp.sum(d_value_all, axis=0, dtype=jnp.float32)
    d_norm1 = rows_sum(
        back_product(d_query_all, w_query)
        + back_product(d_key_all, key_weight)
        + back_product(d_value_all, value_weight)
    )
    grad_inputs = d_middle + norm_backward(inputs_wide, inv_rms1, gain_attn, d_norm1)
    gain_term1 = jnp.sum(d_norm1 * inputs_wide * inv_rms1, axis=0)
    gain_term2 = jnp.sum(d_norm2 * middle * inv_rms2, axis=0)
    gain_sum1, gain_sum2 = lax.psum((gain_term1, gain_term2), "row")
    summed = (
        lax.psum_scatter(
            gain_sum1.astype(jnp.bfloat16), "dp", scatter_dimension=0, tiled=True
        ).astype(jnp.float32),
        lax.psum_scatter(
            grad_query.astype(jnp.bfloat16), "dp", scatter_dimension=0, tiled=True
        ).astype(jnp.float32),
        lax.psum_scatter(
            grad_bias_q.astype(jnp.bfloat16), "dp", scatter_dimension=0, tiled=True
        ).astype(jnp.float32),
        lax.psum_scatter(
            grad_key.astype(jnp.bfloat16), "dp", scatter_dimension=0, tiled=True
        ).astype(jnp.float32),
        lax.psum_scatter(
            grad_bias_k.astype(jnp.bfloat16), "dp", scatter_dimension=0, tiled=True
        ).astype(jnp.float32),
        lax.psum_scatter(
            grad_value.astype(jnp.bfloat16), "dp", scatter_dimension=0, tiled=True
        ).astype(jnp.float32),
        lax.psum_scatter(
            grad_bias_v.astype(jnp.bfloat16), "dp", scatter_dimension=0, tiled=True
        ).astype(jnp.float32),
        lax.psum_scatter(
            grad_output.astype(jnp.bfloat16), "dp", scatter_dimension=0, tiled=True
        ).astype(jnp.float32),
        lax.psum_scatter(
            gain_sum2.astype(jnp.bfloat16), "dp", scatter_dimension=0, tiled=True
        ).astype(jnp.float32),
        lax.psum_scatter(
            grad_gate.astype(jnp.bfloat16), "dp", scatter_dimension=0, tiled=True
        ).astype(jnp.float32),
        lax.psum_scatter(
            grad_up.astype(jnp.bfloat16), "dp", scatter_dimension=0, tiled=True
        ).astype(jnp.float32),
        lax.psum_scatter(
            grad_down.astype(jnp.bfloat16), "dp", scatter_dimension=0, tiled=True
        ).astype(jnp.float32),
    )
    return (outputs.astype(jnp.bfloat16), grad_inputs.astype(jnp.bfloat16)) + tuple(summed)


def solution(mesh):
    return jax.shard_map(
        shards,
        mesh=mesh,
        in_specs=(
            P(("dp", "row"), "col"),
            P(("col", "dp")),
            P(("col", "dp"), "row"),
            P(("row", "dp")),
            P(("col", "dp"), "row"),
            P(("row", "dp")),
            P(("col", "dp"), "row"),
            P(("row", "dp")),
            P(("row", "dp"), "col"),
            P(("col", "dp")),
            P(("col", "dp"), "row"),
            P(("col", "dp"), "row"),
            P(("row", "dp"), "col"),
            P(("dp", "row"), "col"),
        ),
        out_specs=(
            P(("dp", "row"), "col"),
            P(("dp", "row"), "col"),
            P(("col", "dp")),
            P(("col", "dp"), "row"),
            P(("row", "dp")),
            P(("col", "dp"), "row"),
            P(("row", "dp")),
            P(("col", "dp"), "row"),
            P(("row", "dp")),
            P(("row", "dp"), "col"),
            P(("col", "dp")),
            P(("col", "dp"), "row"),
            P(("col", "dp"), "row"),
            P(("row", "dp"), "col"),
        ),
        check_vma=False,
    )
```

profile of v0, /device:TPU:0, one launch (start us, length us, event | category | flops | bytes accessed | tf_op | source)
XLA Modules:
  0.0 1543.1 jit_solution(1339654693611633211)
XLA Ops:
  14.8 13.7 all-reduce.12
  29.6 5.7 psum.42
  36.5 11.5 all_gather.76
  48.0 16.3 %all_gather.77 = bf16[384,768]{1,0:T(8,128)(2,1)S(1)} all-gather(bf16[96,768]{1,0:T(8,128)(2,1)} %param.16), channel_id=1, replica_groups=mesh['dp'=4,'row'=2,'col'=4] {'dp'}, dimensions={0}, use_global_device_ids=true | all-gather | bytes 737280 | tf_op jit(solution)/shard_map/all_gather | solution.py:172
  64.3 13.6 all_gather.78
  77.9 13.5 all_gather.79
  96.2 41.1 %reduce-scatter.18.cloned.1.call-done = f32[256,1024]{0,1:T(8,128)} async-done(((f32[1024,1024]{0,1:T(8,128)}), f32[256,1024]{0,1:T(8,128)}) %reduce-scatter.18.cloned.1.call-update) | async-done | bytes 1048592 | tf_op jit(solution)/shard_map/reduce_scatter | solution.py:80
  139.8 5.8 all-gather
  145.5 5.8 all_gather.83
  157.5 17.3 %all_gather.86 = bf16[768,384]{1,0:T(8,128)(2,1)S(1)} all-gather(bf16[192,384]{1,0:T(8,128)(2,1)S(1)} %copy-done.25), channel_id=1, replica_groups=mesh['dp'=4,'row'=2,'col'=4] {'dp'}, dimensions={0}, use_global_device_ids=true | all-gather | bytes 737280 | tf_op jit(solution)/shard_map/all_gather | solution.py:178
  181.5 12.1 all_gather.93
  193.6 53.0 %all-gather.19.cloned.1.call-done = bf16[4480,384]{1,0:T(8,128)(2,1)} async-done(((bf16[1120,384]{1,0:T(8,128)(2,1)}), bf16[4480,384]{1,0:T(8,128)(2,1)}) %all-gather.19.cloned.1.call-update) | async-done | bytes 3440656 | tf_op jit(solution)/shard_map/all_gather | solution.py:182
  246.6 11.0 fusion.81
  257.6 16.4 %reduce-scatter.20.cloned.1.call-done = f32[512,384]{1,0:T(8,128)} async-done(((f32[1024,384]{1,0:T(8,128)}), f32[512,384]{1,0:T(8,128)}) %reduce-scatter.20.cloned.1.call-update) | async-done | bytes 786448 | tf_op jit(solution)/shard_map/reduce_scatter | solution.py:70
  275.3 6.4 psum.43
  281.9 10.8 all_gather.88
  292.7 51.1 %all-gather.13.cloned.1.call-done = bf16[384,4480]{1,0:T(8,128)(2,1)} async-done(((bf16[96,4480]{1,0:T(8,128)(2,1)}), bf16[384,4480]{1,0:T(8,128)(2,1)}) %all-gather.13.cloned.1.call-update) | async-done | bytes 3440656 | tf_op jit(solution)/shard_map/all_gather | solution.py:180
  343.8 68.4 %all-gather.15.cloned.1.call-done = bf16[384,4480]{1,0:T(8,128)(2,1)} async-done(((bf16[96,4480]{1,0:T(8,128)(2,1)}), bf16[384,4480]{1,0:T(8,128)(2,1)}) %all-gather.15.cloned.1.call-update) | async-done | bytes 3440656 | tf_op jit(solution)/shard_map/all_gather | solution.py:181
  412.2 26.8 %fusion = f32[1024,8960]{1,0:T(8,128)} fusion(bf16[1024,384]{1,0:T(8,128)(2,1)S(1)} %all_gather.88, bf16[384,4480]{1,0:T(8,128)(2,1)} %all-gather.15.cloned.1.call-done, bf16[384,4480]{1,0:T(8,128)(2,1)} %all-gather.13.cloned.1.call-done), kind=kOutput, calls=%fused_computation.3 | convolution fusion | flops 7060193280 | bytes 44367872 | tf_op jit(solution)/shard_map/dot_general | solution.py:76
  439.1 109.0 %reduce-scatter.26.cloned.1.call-done = f32[256,4480]{1,0:T(8,128)} async-done(((f32[1024,4480]{1,0:T(8,128)}), f32[256,4480]{1,0:T(8,128)}) %reduce-scatter.26.cloned.1.call-update) | async-done | bytes 4587536 | tf_op jit(solution)/shard_map/reduce_scatter | solution.py:80
  548.0 253.9 %reduce-scatter.22.cloned.1.call-done = f32[256,8960]{1,0:T(8,128)} async-done(((f32[1024,8960]{1,0:T(8,128)}), f32[256,8960]{1,0:T(8,128)}) %reduce-scatter.22.cloned.1.call-update) | async-done | bytes 9175056 | tf_op jit(solution)/shard_map/reduce_scatter | solution.py:80
  801.9 7.8 multiply_convert_fusion
  811.1 61.5 %all-gather.21.cloned.1.call-done = bf16[1024,4480]{1,0:T(8,128)(2,1)} async-done(((bf16[256,4480]{1,0:T(8,128)(2,1)}), bf16[1024,4480]{1,0:T(8,128)(2,1)}) %all-gather.21.cloned.1.call-update) | async-done | bytes 9175056 | tf_op jit(solution)/shard_map/all_gather | solution.py:64
  872.6 9.4 fusion.82
  882.0 54.8 %all-gather.23.cloned.1.call-done = bf16[1024,4480]{1,0:T(8,128)(2,1)} async-done(((bf16[256,4480]{1,0:T(8,128)(2,1)}), bf16[1024,4480]{1,0:T(8,128)(2,1)}) %all-gather.23.cloned.1.call-update) | async-done | bytes 9175056 | tf_op jit(solution)/shard_map/all_gather | solution.py:64
  936.8 9.7 convolution_add_fusion
  946.6 54.6 %all-gather.17.cloned.1.call-done = bf16[1024,4480]{1,0:T(8,128)(2,1)} async-done(((bf16[256,4480]{1,0:T(8,128)(2,1)}), bf16[1024,4480]{1,0:T(8,128)(2,1)}) %all-gather.17.cloned.1.call-update) | async-done | bytes 9175056 | tf_op jit(solution)/shard_map/all_gather | solution.py:64
  1001.1 9.4 fusion.80
  1010.6 19.4 %reduce-scatter.28.cloned.1.call-done = f32[512,384]{1,0:T(8,128)} async-done(((f32[1024,384]{1,0:T(8,128)}), f32[512,384]{1,0:T(8,128)}) %reduce-scatter.28.cloned.1.call-update) | async-done | bytes 786448 | tf_op jit(solution)/shard_map/reduce_scatter | solution.py:70
  1032.0 6.6 psum.44
  1038.6 20.4 %reduce-scatter.24.cloned.1.call-done = f32[512,384]{1,0:T(8,128)} async-done(((f32[1024,384]{1,0:T(8,128)}), f32[512,384]{1,0:T(8,128)}) %reduce-scatter.24.cloned.1.call-update) | async-done | bytes 786448 | tf_op jit(solution)/shard_map/reduce_scatter | solution.py:70
  1061.7 11.3 all_gather.96
  1076.8 38.0 %reduce-scatter.30.cloned.1.call-done = f32[256,768]{1,0:T(8,128)} async-done(((f32[1024,768]{1,0:T(8,128)}), f32[256,768]{1,0:T(8,128)}) %reduce-scatter.30.cloned.1.call-update) | async-done | bytes 786448 | tf_op jit(solution)/shard_map/reduce_scatter | solution.py:80
  1140.3 9.1 convolution_convert_fusion
  1149.4 9.2 convolution_convert_fusion.1
  1159.0 10.0 convolution_convert_fusion.2
  1170.1 5.8 all_gather.99
  1177.1 7.8 all-gather.1
  1200.3 15.2 reduce-scatter.44.cloned.1.call-done
  1217.1 64.1 %reduce-scatter.48.cloned.1.call-done = bf16[96,4480]{1,0:T(8,128)(2,1)} async-done(((bf16[384,4480]{1,0:T(8,128)(2,1)}), bf16[96,4480]{1,0:T(8,128)(2,1)}) %reduce-scatter.48.cloned.1.call-update) | async-done | bytes 860176 | tf_op jit(solution)/shard_map/reduce_scatter | solution.py:292
  1283.7 64.8 %reduce-scatter.46.cloned.1.call-done = bf16[96,4480]{1,0:T(8,128)(2,1)} async-done(((bf16[384,4480]{1,0:T(8,128)(2,1)}), bf16[96,4480]{1,0:T(8,128)(2,1)}) %reduce-scatter.46.cloned.1.call-update) | async-done | bytes 860176 | tf_op jit(solution)/shard_map/reduce_scatter | solution.py:289
  1351.0 65.0 %reduce-scatter.50.cloned.1.call-done = bf16[1120,384]{1,0:T(8,128)(2,1)} async-done(((bf16[4480,384]{1,0:T(8,128)(2,1)}), bf16[1120,384]{1,0:T(8,128)(2,1)}) %reduce-scatter.50.cloned.1.call-update) | async-done | bytes 860176 | tf_op jit(solution)/shard_map/reduce_scatter | solution.py:295
  1418.7 19.0 %reduce-scatter.42.cloned.1.call-done = bf16[96,128]{1,0:T(8,128)(2,1)} async-done(((bf16[384,128]{1,0:T(8,128)(2,1)}), bf16[96,128]{1,0:T(8,128)(2,1)}) %reduce-scatter.42.cloned.1.call-update) | async-done | bytes 24592 | tf_op jit(solution)/shard_map/reduce_scatter | solution.py:277
  1439.1 19.0 %reduce-scatter.40.cloned.1.call-done = bf16[96,128]{1,0:T(8,128)(2,1)} async-done(((bf16[384,128]{1,0:T(8,128)(2,1)}), bf16[96,128]{1,0:T(8,128)(2,1)}) %reduce-scatter.40.cloned.1.call-update) | async-done | bytes 24592 | tf_op jit(solution)/shard_map/reduce_scatter | solution.py:271
  1459.8 20.9 %reduce-scatter.38.cloned.1.call-done = bf16[96,768]{1,0:T(8,128)(2,1)} async-done(((bf16[384,768]{1,0:T(8,128)(2,1)}), bf16[96,768]{1,0:T(8,128)(2,1)}) %reduce-scatter.38.cloned.1.call-update) | async-done | bytes 147472 | tf_op jit(solution)/shard_map/reduce_scatter | solution.py:265
  1482.3 25.2 %reduce-scatter.36.cloned.1.call-done = f32[512,384]{1,0:T(8,128)} async-done(((f32[1024,384]{1,0:T(8,128)}), f32[512,384]{1,0:T(8,128)}) %reduce-scatter.36.cloned.1.call-update) | async-done | bytes 786448 | tf_op jit(solution)/shard_map/reduce_scatter | solution.py:70
  1509.0 6.4 psum.45
  1520.3 11.8 all-reduce.11
  (196 shorter events, 104.8 us)
Async XLA Ops:
  7.2 130.1 %reduce-scatter.18.cloned.1.call-start = ((), (), s32[]{:S(2)}) async-start(), calls=%async_computation.17 | async-start | bytes 5242880 | tf_op jit(solution)/shard_map/reduce_scatter | solution.py:80
  48.0 43.3 %copy-start.1 = (bf16[1024,384]{1,0:T(8,128)(2,1)}, bf16[1024,384]{1,0:T(8,128)(2,1)S(1)}, u32[]{:S(2)}) copy-start(bf16[1024,384]{1,0:T(8,128)(2,1)S(1)} %all_gather.76) | copy-start | bytes 2359300
  64.3 27.1 %copy-start.16 = (bf16[384,768]{1,0:T(8,128)(2,1)}, bf16[384,768]{1,0:T(8,128)(2,1)S(1)}, u32[]{:S(2)}) copy-start(bf16[384,768]{1,0:T(8,128)(2,1)S(1)} %all_gather.77) | copy-start | bytes 1769476
  77.9 16.8 %copy-start.23 = (bf16[384,128]{1,0:T(8,128)(2,1)}, bf16[384,128]{1,0:T(8,128)(2,1)S(1)}, u32[]{:S(2)}) copy-start(bf16[384,128]{1,0:T(8,128)(2,1)S(1)} %all_gather.78) | copy-start | bytes 294916
  94.7 82.0 %all-gather.11.cloned.1.call-start = ((), (), s32[]{:S(2)}) async-start(), calls=%async_computation.18 | async-start | bytes 1966080 | tf_op jit(solution)/shard_map/all_gather | solution.py:64
  94.7 50.8 %copy-start.29 = (f32[64]{0:T(128)}, f32[64]{0:T(128)S(1)}, u32[]{:S(2)}) copy-start(f32[64]{0:T(128)S(1)} %negate_power_fusion) | copy-start | bytes 772
  94.8 50.8 %copy-start.26 = (f32[256]{0:T(256)}, f32[256]{0:T(256)S(1)}, u32[]{:S(2)}) copy-start(f32[256]{0:T(256)S(1)} %fusion.70) | copy-start | bytes 3076
  96.2 55.4 %copy-start.20 = (f32[256,64]{1,0:T(8,128)}, f32[256,64]{1,0:T(8,128)S(1)}, u32[]{:S(2)}) copy-start(f32[256,64]{1,0:T(8,128)S(1)} %get-tuple-element.50) | copy-start | bytes 196612
  145.5 8.2 copy-start.15
  156.7 89.9 %all-gather.19.cloned.1.call-start = ((), (), s32[]{:S(2)}) async-start(), calls=%async_computation.24 | async-start | bytes 4300800 | tf_op jit(solution)/shard_map/all_gather | solution.py:182
  157.4 116.6 %reduce-scatter.20.cloned.1.call-start = ((), (), s32[]{:S(2)}) async-start(), calls=%async_computation.19 | async-start | bytes 2359296 | tf_op jit(solution)/shard_map/reduce_scatter | solution.py:70
  174.8 6.7 copy-start.19
  180.3 163.5 %all-gather.13.cloned.1.call-start = ((), (), s32[]{:S(2)}) async-start(), calls=%async_computation.20 | async-start | bytes 4300800 | tf_op jit(solution)/shard_map/all_gather | solution.py:180
  180.8 231.3 %all-gather.15.cloned.1.call-start = ((), (), s32[]{:S(2)}) async-start(), calls=%async_computation.21 | async-start | bytes 4300800 | tf_op jit(solution)/shard_map/all_gather | solution.py:181
  181.4 366.6 %reduce-scatter.26.cloned.1.call-start = ((), (), s32[]{:S(2)}) async-start(), calls=%async_computation.26 | async-start | bytes 22937600 | tf_op jit(solution)/shard_map/reduce_scatter | solution.py:80
  193.6 64.0 %copy-start.6 = (bf16[1024,384]{1,0:T(8,128)(2,1)}, bf16[1024,384]{1,0:T(8,128)(2,1)S(1)}, u32[]{:S(2)}) copy-start(bf16[1024,384]{1,0:T(8,128)(2,1)S(1)} %all_gather.93) | copy-start | bytes 2359300
  257.6 16.5 %copy-start.5 = (bf16[512,384]{1,0:T(8,128)(2,1)S(1)}, bf16[512,384]{1,0:T(8,128)(2,1)}, u32[]{:S(2)}) copy-start(bf16[512,384]{1,0:T(8,128)(2,1)} %param.14) | copy-start | bytes 1179652
  257.6 544.3 %reduce-scatter.22.cloned.1.call-start = ((), (), s32[]{:S(2)}) async-start(), calls=%async_computation.22 | async-start | bytes 45875200 | tf_op jit(solution)/shard_map/reduce_scatter | solution.py:80
  292.7 146.3 %copy-start.3 = (bf16[1024,384]{1,0:T(8,128)(2,1)}, bf16[1024,384]{1,0:T(8,128)(2,1)S(1)}, u32[]{:S(2)}) copy-start(bf16[1024,384]{1,0:T(8,128)(2,1)S(1)} %all_gather.88) | copy-start | bytes 2359300
  439.0 433.6 %all-gather.21.cloned.1.call-start = ((), (), s32[]{:S(2)}) async-start(), calls=%async_computation.27 | async-start | bytes 11468800 | tf_op jit(solution)/shard_map/all_gather | solution.py:64
  809.7 127.0 %all-gather.23.cloned.1.call-start = ((), (), s32[]{:S(2)}) async-start(), calls=%async_computation.28 | async-start | bytes 11468800 | tf_op jit(solution)/shard_map/all_gather | solution.py:64
  810.3 190.8 %all-gather.17.cloned.1.call-start = ((), (), s32[]{:S(2)}) async-start(), calls=%async_computation.23 | async-start | bytes 11468800 | tf_op jit(solution)/shard_map/all_gather | solution.py:64
  811.1 218.9 %reduce-scatter.28.cloned.1.call-start = ((), (), s32[]{:S(2)}) async-start(), calls=%async_computation.29 | async-start | bytes 2359296 | tf_op jit(solution)/shard_map/reduce_scatter | solution.py:70
  946.5 112.5 %reduce-scatter.24.cloned.1.call-start = ((), (), s32[]{:S(2)}) async-start(), calls=%async_computation.25 | async-start | bytes 2359296 | tf_op jit(solution)/shard_map/reduce_scatter | solution.py:70
  1010.5 104.3 %reduce-scatter.30.cloned.1.call-start = ((), (), s32[]{:S(2)}) async-start(), calls=%async_computation.30 | async-start | bytes 3932160 | tf_op jit(solution)/shard_map/reduce_scatter | solution.py:80
  1076.7 92.4 %reduce-scatter.34.cloned.1.call-start = ((), (), s32[]{:S(2)}) async-start(), calls=%async_computation.33 | async-start | bytes 655360 | tf_op jit(solution)/shard_map/reduce_scatter | solution.py:240
  1120.9 54.9 %reduce-scatter.32.cloned.1.call-start = ((), (), s32[]{:S(2)}) async-start(), calls=%async_computation.32 | async-start | bytes 655360 | tf_op jit(solution)/shard_map/reduce_scatter | solution.py:239
  1125.0 4.7 copy-start.9
  1125.0 4.7 copy-start.11
  1132.0 58.6 %all-gather.25.cloned.1.call-start = ((), (), s32[]{:S(2)}) async-start(), calls=%async_computation.31 | async-start | bytes 1966080 | tf_op jit(solution)/shard_map/all_gather | solution.py:64
  1135.7 4.5 copy-start.4
  1136.9 78.6 %reduce-scatter.44.cloned.1.call-start = ((), (), s32[]{:S(2)}) async-start(), calls=%async_computation.38 | async-start | bytes 737280 | tf_op jit(solution)/shard_map/reduce_scatter | solution.py:283
  1140.2 141.0 %reduce-scatter.48.cloned.1.call-start = ((), (), s32[]{:S(2)}) async-start(), calls=%async_computation.40 | async-start | bytes 4300800 | tf_op jit(solution)/shard_map/reduce_scatter | solution.py:292
  1149.4 9.6 copy-start.7
  1149.4 199.2 %reduce-scatter.46.cloned.1.call-start = ((), (), s32[]{:S(2)}) async-start(), calls=%async_computation.39 | async-start | bytes 4300800 | tf_op jit(solution)/shard_map/reduce_scatter | solution.py:289
  1158.7 17.2 %copy-start.27 = (f32[256]{0:T(256)S(1)}, f32[256]{0:T(256)}, u32[]{:S(2)}) copy-start(f32[256]{0:T(256)} %copy-done.26) | copy-start | bytes 3076
  1158.7 17.2 %copy-start.30 = (f32[64]{0:T(128)S(1)}, f32[64]{0:T(128)}, u32[]{:S(2)}) copy-start(f32[64]{0:T(128)} %copy-done.29) | copy-start | bytes 772
  1158.7 257.3 %reduce-scatter.50.cloned.1.call-start = ((), (), s32[]{:S(2)}) async-start(), calls=%async_computation.41 | async-start | bytes 4300800 | tf_op jit(solution)/shard_map/reduce_scatter | solution.py:295
  1169.0 15.9 %copy-start.2 = (bf16[1024,384]{1,0:T(8,128)(2,1)S(1)}, bf16[1024,384]{1,0:T(8,128)(2,1)}, u32[]{:S(2)}) copy-start(bf16[1024,384]{1,0:T(8,128)(2,1)} %copy-done.1) | copy-start | bytes 2359300
  1169.0 24.7 %copy-start.24 = (bf16[384,128]{1,0:T(8,128)(2,1)S(1)}, bf16[384,128]{1,0:T(8,128)(2,1)}, u32[]{:S(2)}) copy-start(bf16[384,128]{1,0:T(8,128)(2,1)} %copy-done.23) | copy-start | bytes 294916
  1169.0 268.7 %reduce-scatter.42.cloned.1.call-start = ((), (), s32[]{:S(2)}) async-start(), calls=%async_computation.37 | async-start | bytes 122880 | tf_op jit(solution)/shard_map/reduce_scatter | solution.py:277
  1177.1 17.1 %copy-start.17 = (bf16[384,768]{1,0:T(8,128)(2,1)S(1)}, bf16[384,768]{1,0:T(8,128)(2,1)}, u32[]{:S(2)}) copy-start(bf16[384,768]{1,0:T(8,128)(2,1)} %copy-done.16) | copy-start | bytes 1769476
  1186.0 272.2 %reduce-scatter.40.cloned.1.call-start = ((), (), s32[]{:S(2)}) async-start(), calls=%async_computation.36 | async-start | bytes 122880 | tf_op jit(solution)/shard_map/reduce_scatter | solution.py:271
  1187.1 293.5 %reduce-scatter.38.cloned.1.call-start = ((), (), s32[]{:S(2)}) async-start(), calls=%async_computation.35 | async-start | bytes 737280 | tf_op jit(solution)/shard_map/reduce_scatter | solution.py:265
  1193.7 313.8 %reduce-scatter.36.cloned.1.call-start = ((), (), s32[]{:S(2)}) async-start(), calls=%async_computation.34 | async-start | bytes 2359296 | tf_op jit(solution)/shard_map/reduce_scatter | solution.py:70
  1198.2 261.3 %copy-start.18 = (bf16[1024,768]{0,1:T(8,128)(2,1)S(1)}, bf16[1024,768]{0,1:T(8,128)(2,1)}, u32[]{:S(2)}) copy-start(bf16[1024,768]{0,1:T(8,128)(2,1)} %all-gather.25.cloned.1.call-done) | copy-start | bytes 4718596
  1283.7 231.7 %copy-start.28 = (f32[384]{0:T(512)S(1)}, f32[384]{0:T(512)}, u32[]{:S(2)}) copy-start(f32[384]{0:T(512)} %get-tuple-element.14) | copy-start | bytes 4612
  1283.7 250.2 %copy-start.12 = (f32[512,384]{1,0:T(8,128)S(1)}, f32[512,384]{1,0:T(8,128)}, u32[]{:S(2)}) copy-start(f32[512,384]{1,0:T(8,128)} %get-tuple-element.31) | copy-start | bytes 2359300
  (8 other events, 19.2 us)
Sparse Core Ops, SparseCore 0:
  94.8 42.4 reduce-scatter.17
  156.8 19.8 all-gather.10
  178.2 68.2 all-gather.18
  249.3 24.7 reduce-scatter.19
  275.5 68.3 all-gather.12
  345.2 66.8 all-gather.14
  414.8 133.1 reduce-scatter.25
  550.6 251.2 reduce-scatter.21
  809.9 62.7 all-gather.20
  874.0 62.7 all-gather.22
  938.4 62.7 all-gather.16
  1003.8 26.1 reduce-scatter.27
  1032.8 26.1 reduce-scatter.23
  1076.8 37.9 reduce-scatter.29
  1121.0 21.6 reduce-scatter.33
  1145.7 21.6 reduce-scatter.31
  1169.3 21.2 all-gather.24
  1193.3 22.1 reduce-scatter.43
  1217.8 63.3 reduce-scatter.47
  1283.4 65.0 reduce-scatter.45
  1350.8 65.1 reduce-scatter.49
  1418.2 19.4 reduce-scatter.41
  1440.6 17.5 reduce-scatter.39
  1460.3 20.3 reduce-scatter.37
  1482.9 24.5 reduce-scatter.35
where the time goes:
time: 1550 us; the launch traced here: 1540 us
  waiting for transfers between devices  1140 us (74%)
  blocking collectives  187 us (12%)
  matrix products  134 us (9%)
  other arithmetic  49.6 us (3%)
  between operations  19.1 us (1%)
    reduce_scatter x4, waiting for transfers between devices, width_sum(): lax.psum_scatter(term(jnp.int32(0), lax.axis_size('col') * (whole.shape[0...  442 us
    all_gather x5, waiting for transfers between devices, cols_whole(): lax.all_gather(shortened(local), 'col', axis=0, tiled=True)  176 us
    reduce_scatter x4, waiting for transfers between devices, rows_sum(): return lax.psum_scatter(term, 'row', scatter_dimension=0, tiled=True)  81.4 us
    all_gather x1, waiting for transfers between devices, shards(): lax.all_gather(w_up, 'dp', axis=0, tiled=True)  68.4 us
    reduce_scatter x1, waiting for transfers between devices, shards(): lax.psum_scatter(grad_down.astype(jnp.bfloat16), 'dp', scatter_dimension=...  65 us
    reduce_scatter x1, waiting for transfers between devices, shards(): lax.psum_scatter(grad_gate.astype(jnp.bfloat16), 'dp', scatter_dimension=...  64.8 us
    reduce_scatter x1, waiting for transfers between devices, shards(): lax.psum_scatter(grad_up.astype(jnp.bfloat16), 'dp', scatter_dimension=0,...  64.1 us
    all_gather x1, waiting for transfers between devices, shards(): lax.all_gather(w_down, 'dp', axis=0, tiled=True)  53 us
  transfers between devices with their start and end apart: 25, of which 23 were waited for; matrix products, arithmetic and copies ran while one was open for 10% of the time, Pallas kernels for 0%

commit v1 on v0

v1 whole, which is shorter than its diff:
```python
import math

import jax
import jax.numpy as jnp
from jax import lax
from jax.sharding import Mesh, PartitionSpec as P

HEAD = 128
EPS = 1e-06
ROPE_BASE = 1000000.0
F32 = jnp.float32
BF16 = jnp.bfloat16


def rope(rows, positions, direction):
    half = HEAD // 2
    n = rows.shape[0]
    heads = rows.shape[1] // HEAD
    freqs = ROPE_BASE ** (-(jnp.arange(half, dtype=F32) * 2.0 / HEAD))
    angles = positions.astype(F32)[:, None] * freqs[None, :]
    cosine = jnp.cos(angles)[:, None, :]
    sine = direction * jnp.sin(angles)[:, None, :]
    shaped = rows.reshape(n, heads, HEAD)
    a = shaped[..., :half]
    b = shaped[..., half:]
    turned = jnp.concatenate([a * cosine - b * sine, b * cosine + a * sine], -1)
    return turned.reshape(n, heads * HEAD)


def nn(a, b):
    return lax.dot_general(a, b, (((1,), (0,)), ((), ())), preferred_element_type=F32)


def nt(a, b):
    return lax.dot_general(a, b, (((1,), (1,)), ((), ())), preferred_element_type=F32)


def tn(a, b):
    return lax.dot_general(a, b, (((0,), (0,)), ((), ())), preferred_element_type=F32)


def shards(x, g1, wq, bq, wk, bk, wv, bv, wo, g2, wg, wu, wd, cot):
    pods, D, R, C = (lax.axis_size(a) for a in ("pod", "dp", "row", "col"))
    width = x.shape[1] * C
    rows_f = g1.shape[0]
    tok = x.shape[0] // C
    qw, kw = wq.shape[1], wk.shape[1]
    heads, kv = qw // HEAD, kw // HEAD
    units_r = wg.shape[1]
    both = jnp.concatenate([x, cot], 1).reshape(C, tok, 2 * x.shape[1])
    both = lax.all_to_all(both, "col", 0, 0, tiled=True).reshape(C, tok, 2, x.shape[1])
    both = both.transpose(2, 1, 0, 3).reshape(2, tok, width)
    x_own, cot_own = both[0], both[1]
    x_pair = lax.all_gather(x_own, "row", axis=0, tiled=True)
    bias = jnp.concatenate([bq, bk, bv])
    nb = -(-bias.shape[0] // rows_f)
    bias_cols = jnp.pad(bias, (0, nb * rows_f - bias.shape[0])).reshape(nb, rows_f).T
    pack = jnp.concatenate([wq, wk, wv, g1[:, None], g2[:, None], bias_cols], 1)
    pack = lax.all_gather(pack, ("col", "pod", "dp"), axis=0, tiled=True)
    ow = qw + 2 * kw
    w_in = pack[:, :ow]
    gain1 = pack[:, ow].astype(F32)
    gain2 = pack[:, ow + 1].astype(F32)
    b_all = pack[: width // C, ow + 2 :].reshape(pods * D, rows_f, nb).transpose(0, 2, 1)
    b_all = b_all.reshape(pods * D, nb * rows_f)
    lq, lk = bq.shape[0], bk.shape[0]
    bias_in = jnp.concatenate(
        [
            b_all[:, :lq].reshape(-1),
            b_all[:, lq : lq + lk].reshape(-1),
            b_all[:, lq + lk : lq + 2 * lk].reshape(-1),
        ]
    ).astype(F32)
    w_out = lax.all_gather(wo, ("pod", "dp", "col"), axis=0)
    w_out = w_out.reshape(pods * D, C, wo.shape[0], wo.shape[1]).transpose(0, 2, 1, 3)
    w_out = w_out.reshape(qw, width)
    if pods > 1:
        wg, wu, wd = (lax.all_gather(w, "pod", axis=0) for w in (wg, wu, wd))
    else:
        wg, wu, wd = wg[None], wu[None], wd[None]
    share = units_r // (D * C)

    def spread(w):
        u = units_r // (pods * D)
        w = w.reshape(pods, rows_f, pods, D, u).transpose(3, 2, 4, 0, 1).reshape(D, C, share, pods, rows_f)
        return w.transpose(1, 0, 3, 4, 2)

    gu = jnp.concatenate([spread(wg), spread(wu)], -1)
    gu = gu.reshape(C * D, pods, rows_f, 2 * share)
    gu = lax.all_to_all(gu, ("col", "dp"), 0, 0, tiled=True)
    gu = gu.reshape(C, D, pods, rows_f, 2 * share).transpose(0, 2, 1, 3, 4).reshape(width, 2 * share)
    gu = lax.all_gather(gu, "row", axis=0)
    w_g = jnp.concatenate([gu[i, :, :share] for i in range(R)], 1)
    w_u = jnp.concatenate([gu[i, :, share:] for i in range(R)], 1)
    dn = wd.reshape(C, share, wd.shape[2])
    dn = lax.all_to_all(dn, "col", 0, 0, tiled=True).transpose(1, 0, 2).reshape(share, width)
    w_d = lax.all_gather(dn, "row", axis=0, tiled=True)
    cot_all = lax.all_gather(cot_own, ("dp", "col"), axis=0, tiled=True)
    c = lax.axis_index("col")
    sub = jnp.arange(tok, dtype=jnp.int32)
    positions = (jnp.arange(R, dtype=jnp.int32)[:, None] * (tok * C) + c * tok + sub[None, :]).reshape(-1)
    key_pos = (
        jnp.arange(C, dtype=jnp.int32)[:, None, None] * tok
        + jnp.arange(R, dtype=jnp.int32)[None, :, None] * (tok * C)
        + sub[None, None, :]
    ).reshape(-1)
    xp = x_pair.astype(F32)
    inv1 = lax.rsqrt(jnp.mean(xp * xp, 1, keepdims=True) + EPS)
    normed1 = (xp * inv1 * gain1).astype(BF16)
    proj = nn(normed1, w_in) + bias_in
    q = rope(proj[:, :qw], positions, 1.0).astype(BF16)
    k = rope(proj[:, qw : qw + kw], positions, 1.0).astype(BF16)
    v = proj[:, qw + kw :].astype(BF16)
    kv_all = lax.all_gather(jnp.concatenate([k, v], 1), "col", axis=0, tiled=True)
    ka, va = kv_all[:, :kw], kv_all[:, kw:]
    nq = q.shape[0]
    ns = ka.shape[0]
    group = heads // kv
    q4 = q.reshape(nq, kv, group, HEAD)
    k3 = ka.reshape(ns, kv, HEAD)
    v3 = va.reshape(ns, kv, HEAD)
    scores = jnp.einsum("ikgd,jkd->kgij", q4, k3, preferred_element_type=F32) * HEAD ** (-0.5)
    admitted = key_pos[None, :] <= positions[:, None]
    scores = jnp.where(admitted, scores, -1e30)
    top = jnp.max(scores, -1, keepdims=True)
    expo = jnp.exp(scores - top)
    total = jnp.sum(expo, -1, keepdims=True)
    probs = expo / total
    probs_low = probs.astype(BF16)
    att = jnp.einsum("kgij,jkd->ikgd", probs_low, v3, preferred_element_type=F32)
    att = att.reshape(nq, qw).astype(BF16)
    part = nn(att, w_out).astype(BF16)
    mid = x_own.astype(F32) + lax.psum_scatter(part, "row", scatter_dimension=0, tiled=True).astype(F32)
    inv2 = lax.rsqrt(jnp.mean(mid * mid, 1, keepdims=True) + EPS)
    normed2 = (mid * inv2 * gain2).astype(BF16)
    n2 = lax.all_gather(normed2, ("dp", "col"), axis=0, tiled=True)
    gate = nn(n2, w_g)
    up = nn(n2, w_u)
    d_hidden = nt(cot_all, w_d)
    sig = jax.nn.sigmoid(gate)
    silu = gate * sig
    hidden = (silu * up).astype(BF16)
    d_gate = (d_hidden * up * sig * (1.0 + gate * (1.0 - sig))).astype(BF16)
    d_up = (d_hidden * silu).astype(BF16)
    d_n2 = (nt(d_gate, w_g) + nt(d_up, w_u)).astype(BF16)
    d_n2 = lax.psum_scatter(d_n2, ("dp", "col"), scatter_dimension=0, tiled=True).astype(F32)
    out_part = nn(hidden, w_d).astype(BF16)
    out_sum = lax.psum_scatter(out_part, ("dp", "col"), scatter_dimension=0, tiled=True)
    outputs = (mid + out_sum.astype(F32)).astype(BF16)
    g_down = tn(hidden, cot_all).astype(BF16)
    g_gate = tn(n2, d_gate).astype(BF16)
    g_up = tn(n2, d_up).astype(BF16)
    g_gu = jnp.stack(
        [
            jnp.concatenate([g_gate[:, i * share : (i + 1) * share], g_up[:, i * share : (i + 1) * share]], 1)
            for i in range(R)
        ]
    )
    g_gu = lax.psum_scatter(g_gu, "row", scatter_dimension=0, tiled=False)
    g_gu = g_gu.reshape(C, pods, D, rows_f, 2 * share).transpose(0, 2, 1, 3, 4).reshape(C * D, pods, rows_f, 2 * share)
    g_gu = lax.all_to_all(g_gu, ("col", "dp"), 0, 0, tiled=True).reshape(C, D, pods, rows_f, 2, share)
    g_dn = lax.psum_scatter(g_down, "row", scatter_dimension=0, tiled=True)
    g_dn = g_dn.reshape(share, C, wd.shape[2]).transpose(1, 0, 2)
    g_dn = lax.all_to_all(g_dn, "col", 0, 0, tiled=True)
    u = units_r // (pods * D)
    g_dn = g_dn.reshape(pods, u, wd.shape[2])

    def unspread(g):
        g = g.transpose(1, 0, 4, 2, 3).reshape(D, pods, u, pods, rows_f)
        return g.transpose(3, 4, 1, 0, 2).reshape(pods, rows_f, units_r)

    gg, gu_ = unspread(g_gu[..., 0, :]), unspread(g_gu[..., 1, :])
    if pods > 1:
        gg, gu_, g_dn = (lax.psum_scatter(t, "pod", scatter_dimension=0, tiled=False) for t in (gg, gu_, g_dn))
    else:
        gg, gu_, g_dn = gg[0], gu_[0], g_dn[0]
    weighted = d_n2 * gain2
    inner = jnp.sum(weighted * mid, 1, keepdims=True)
    cot_f = cot_own.astype(F32)
    d_mid = cot_f + inv2 * weighted - mid * (inv2 * inv2 * inv2) * inner / width
    gain_term2 = jnp.sum(d_n2 * mid * inv2, 0)
    dm_pair = lax.all_gather(d_mid.astype(BF16), "row", axis=0, tiled=True)
    g_wo = tn(att, dm_pair).astype(BF16)
    g_wo = g_wo.reshape(pods * D, wo.shape[0], C, wo.shape[1]).transpose(0, 2, 1, 3)
    g_wo = lax.psum_scatter(
        g_wo.reshape(pods * D * C, wo.shape[0], wo.shape[1]), ("pod", "dp", "col"), scatter_dimension=0, tiled=False
    )
    d_att = nt(dm_pair, w_out).astype(BF16)
    da4 = d_att.reshape(q4.shape)
    d_probs = jnp.einsum("ikgd,jkd->kgij", da4, v3, preferred_element_type=F32)
    centre = jnp.sum(probs * d_probs, -1, keepdims=True)
    d_scores = (probs * (d_probs - centre)).astype(BF16)
    scale = HEAD ** (-0.5)
    d_q = jnp.einsum("kgij,jkd->ikgd", d_scores, k3, preferred_element_type=F32).reshape(nq, qw) * scale
    d_k = jnp.einsum("kgij,ikgd->jkd", d_scores, q4, preferred_element_type=F32).reshape(ns, kw) * scale
    d_v = jnp.einsum("kgij,ikgd->jkd", probs_low, da4, preferred_element_type=F32).reshape(ns, kw)
    dkv = jnp.concatenate([d_k, d_v], 1).astype(BF16)
    dkv = lax.psum_scatter(dkv, "col", scatter_dimension=0, tiled=True).astype(F32)
    d_in = jnp.concatenate(
        [rope(d_q, positions, -1.0), rope(dkv[:, :kw], positions, -1.0), dkv[:, kw:]], 1
    )
    d_in_low = d_in.astype(BF16)
    d_n1 = nt(d_in_low, w_in).astype(BF16)
    d_n1 = lax.psum_scatter(d_n1, "row", scatter_dimension=0, tiled=True).astype(F32)
    xf = x_own.astype(F32)
    inv_own = lax.rsqrt(jnp.mean(xf * xf, 1, keepdims=True) + EPS)
    weighted1 = d_n1 * gain1
    inner1 = jnp.sum(weighted1 * xf, 1, keepdims=True)
    grad_x = (d_mid + inv_own * weighted1 - xf * (inv_own * inv_own * inv_own) * inner1 / width).astype(BF16)
    gain_term1 = jnp.sum(d_n1 * xf * inv_own, 0)
    g_in = tn(normed1, d_in_low).astype(BF16)
    gb = jnp.sum(d_in_low.astype(F32), 0).astype(BF16)
    gb_parts = jnp.concatenate(
        [
            gb[:qw].reshape(pods * D, lq),
            gb[qw : qw + kw].reshape(pods * D, lk),
            gb[qw + kw :].reshape(pods * D, lk),
            jnp.zeros((pods * D, nb * rows_f - bias.shape[0]), BF16),
        ],
        1,
    )
    gb_cols = gb_parts.reshape(1, pods * D, nb, rows_f).transpose(0, 1, 3, 2)
    gb_cols = jnp.broadcast_to(gb_cols, (C, pods * D, rows_f, nb)).reshape(width, nb)
    g_pack = jnp.concatenate(
        [g_in, gain_term1.astype(BF16)[:, None], gain_term2.astype(BF16)[:, None], gb_cols], 1
    )
    g_pack = lax.psum_scatter(g_pack, ("col", "pod", "dp"), scatter_dimension=0, tiled=True).astype(F32)
    gains = lax.psum(g_pack[:, ow : ow + 2], "row")
    g_bias = g_pack[:, ow + 2 :].T.reshape(-1)
    fin = jnp.concatenate([outputs.reshape(tok, C, -1), grad_x.reshape(tok, C, -1)], 2).transpose(1, 0, 2)
    fin = lax.all_to_all(fin, "col", 0, 0, tiled=True).reshape(C * tok, -1)
    fw = x.shape[1]
    return (
        fin[:, :fw],
        fin[:, fw:],
        gains[:, 0],
        g_pack[:, :qw],
        g_bias[:lq],
        g_pack[:, qw : qw + kw],
        g_bias[lq : lq + lk],
        g_pack[:, qw + kw : ow],
        g_bias[lq + lk : lq + 2 * lk],
        g_wo.astype(F32),
        gains[:, 1],
        gg.astype(F32),
        gu_.astype(F32),
        g_dn.astype(F32),
    )


def solution(mesh):
    team = math.gcd(mesh.shape["dp"], 4)
    names = {"dp": ("pod", "dp"), "row": ("row",), "col": ("col",)}
    sizes = (mesh.shape["dp"] // team, team, mesh.shape["row"], mesh.shape["col"])
    grid = Mesh(mesh.devices.reshape(sizes), ("pod", "dp", "row", "col"))

    def spec(*dims):
        return P(*(tuple(n for a in d for n in names[a]) for d in dims))

    act = spec(("dp", "row"), ("col",))
    vec_f = spec(("col", "dp"))
    w_in = spec(("col", "dp"), ("row",))
    vec_r = spec(("row", "dp"))
    w_out = spec(("row", "dp"), ("col",))
    return jax.shard_map(
        shards,
        mesh=grid,
        in_specs=(act, vec_f, w_in, vec_r, w_in, vec_r, w_in, vec_r, w_out, vec_f, w_in, w_in, w_out, act),
        out_specs=(act, act, vec_f, w_in, vec_r, w_in, vec_r, w_in, vec_r, w_out, vec_f, w_in, w_in, w_out),
        check_vma=False,
    )
```

time: 1550 us -> 912 us (0.59)
  waiting for transfers between devices: 1140 us -> 558 us
  blocking collectives: 187 us -> 50.5 us
  local copies, waits for them, and re-layouts: 9.07 us -> 114 us
  matrix products: 134 us -> 104 us
  starting transfers between devices: 1.27 us -> 24.9 us
    reduce_scatter x17 -> x8, waiting for transfers between devices: 791 us -> 199 us  [the longest x1 86.3 us: shards(): lax.psum_scatter(out_part, ('dp', 'col'), scatter_dimension=0, tiled=True)]
    all_gather x12 -> x3, blocking collectives: 132 us -> 30.7 us  [the longest x1 12.3 us: shards(): x_pair = lax.all_gather(x_own, 'row', axis=0, tiled=True)]
    all_gather x8 -> x6, waiting for transfers between devices: 349 us -> 258 us  [the longest x1 64.1 us: shards(): cot_all = lax.all_gather(cot_own, ('dp', 'col'), axis=0, tiled=True)]
    all_to_all x0 -> x5, waiting for transfers between devices: none -> 56 us  [the longest x1 53.1 us: shards(): lax.all_to_all(g_gu, ('col', 'dp'), 0, 0, tiled=True)]
    unnamed x25 -> x16, waiting for transfers between devices: 3.28 us -> 44.3 us
    dot_general x24 -> x21, matrix products: 134 us -> 104 us  [the longest x5 31.8 us: nn(): lax.dot_general(a, b, (((1,), (0,)), ((), ())), preferred_element_type=F32)]
    unnamed x2 -> x0, blocking collectives: 25.5 us -> none
    psum x5 -> x1, blocking collectives: 30 us -> 4.91 us  [shards(): gains = lax.psum(g_pack[:, ow:ow + 2], 'row')]
  transfers between devices with their start and end apart: 25 -> 20, of which waited for: 23 -> 14; matrix products, arithmetic and copies ran while one was open for 10% -> 21% of each run, Pallas kernels for 0% -> 0%
where the time goes in v1:
time: 912 us; the launch traced here: 904 us
  waiting for transfers between devices  558 us (61%)
  local copies, waits for them, and re-layouts  114 us (12%)
  matrix products  104 us (11%)
  blocking collectives  50.5 us (6%)
  other arithmetic  36.7 us (4%)
  starting transfers between devices  24.9 us (3%)
  between operations  15.4 us (2%)
    reduce_scatter x1, waiting for transfers between devices, shards(): lax.psum_scatter(out_part, ('dp', 'col'), scatter_dimension=0, tiled=True)  86.3 us
    reduce_scatter x1, waiting for transfers between devices, shards(): lax.psum_scatter(d_n2, ('dp', 'col'), scatter_dimension=0, tiled=True)  73.5 us
    all_gather x1, waiting for transfers between devices, shards(): cot_all = lax.all_gather(cot_own, ('dp', 'col'), axis=0, tiled=True)  64.1 us
    all_gather x1, waiting for transfers between devices, shards(): n2 = lax.all_gather(normed2, ('dp', 'col'), axis=0, tiled=True)  53.9 us
    all_to_all x1, waiting for transfers between devices, shards(): lax.all_to_all(g_gu, ('col', 'dp'), 0, 0, tiled=True)  53.1 us
    unnamed x16, waiting for transfers between devices  44.3 us
    all_gather x1, waiting for transfers between devices, shards(): pack = lax.all_gather(pack, ('col', 'pod', 'dp'), axis=0, tiled=True)  44.2 us
    all_gather x1, waiting for transfers between devices, shards(): gu = lax.all_gather(gu, 'row', axis=0)  40.7 us
  transfers between devices with their start and end apart: 20, of which 14 were waited for; matrix products, arithmetic and copies ran while one was open for 21% of the time, Pallas kernels for 0%

profile of v1, /device:TPU:0, one launch (start us, length us, event | category | flops | bytes accessed | tf_op | source)
XLA Modules:
  0.0 903.7 jit_solution(12284536221277183685)
XLA Ops:
  14.3 4.3 all-to-all-start
  29.6 2.9 all-to-all-done
  32.5 5.8 all-to-all-start.1
  40.9 12.3 %all_gather.30 = bf16[256,1536]{1,0:T(8,128)(2,1)S(1)} all-gather(bf16[128,1536]{1,0:T(8,128)(2,1)S(1)} %copy.235), channel_id=1, replica_groups=mesh['dp'=4,'row'=2,'col'=4] {'row'}, dimensions={0}, use_global_device_ids=true | all-gather | bytes 1179648 | tf_op jit(solution)/shard_map/all_gather | solution.py:54
  53.5 28.0 %all-gather.18.cloned.1.call-done = bf16[3072,384]{1,0:T(8,128)(2,1)} async-done(((bf16[192,384]{1,0:T(8,128)(2,1)}), bf16[3072,384]{1,0:T(8,128)(2,1)}) %all-gather.18.cloned.1.call-update) | async-done | bytes 2359312 | tf_op jit(solution)/shard_map/all_gather | solution.py:74
  81.4 3.5 copy.193
  85.3 44.2 %all-gather.8.cloned.1.call-done = bf16[1536,1029]{1,0:T(8,128)(2,1)} async-done(((bf16[96,1029]{1,0:T(8,128)(2,1)}), bf16[1536,1029]{1,0:T(8,128)(2,1)}) %all-gather.8.cloned.1.call-update) | async-done | bytes 3161104 | tf_op jit(solution)/shard_map/all_gather | solution.py:59
  132.7 3.6 fusion.23
  137.6 7.6 all_gather.32
  159.9 3.9 copy.198
  163.9 14.9 %all_to_all.30 = bf16[4,280,384]{2,1,0:T(8,128)(2,1)S(1)} all-to-all(bf16[4,280,384]{2,1,0:T(8,128)(2,1)S(1)} %bitcast.290), channel_id=1, replica_groups=mesh['dp'=4,'row'=2,'col'=4] {'col'}, dimensions={0} | all-to-all | bytes 1720320 | tf_op jit(solution)/shard_map/all_to_all | solution.py:96
  185.7 40.7 %all-gather.12.cloned.1.call-done = bf16[2,1536,560]{1,2,0:T(8,128)(2,1)} async-done(((bf16[1,1536,560]{1,2,0:T(8,128)(2,1)}), bf16[2,1536,560]{1,2,0:T(8,128)(2,1)}) %all-gather.12.cloned.1.call-update) | async-done | bytes 3440656 | tf_op jit(solution)/shard_map/all_gather | solution.py:92
  226.4 3.2 slice_bitcast_fusion.3
  229.5 27.7 %all-gather.14.cloned.1.call-done = bf16[560,1536]{1,0:T(8,128)(2,1)} async-done(((bf16[280,1536]{1,0:T(8,128)(2,1)}), bf16[560,1536]{1,0:T(8,128)(2,1)}) %all-gather.14.cloned.1.call-update) | async-done | bytes 1720336 | tf_op jit(solution)/shard_map/all_gather | solution.py:97
  257.2 64.1 %all-gather.16.cloned.1.call-done = bf16[2048,1536]{1,0:T(8,128)(2,1)} async-done(((bf16[128,1536]{1,0:T(8,128)(2,1)}), bf16[2048,1536]{1,0:T(8,128)(2,1)}) %all-gather.16.cloned.1.call-update) | async-done | bytes 6291472 | tf_op jit(solution)/shard_map/all_gather | solution.py:98
  321.4 9.1 %fusion.108 = f32[2048,560]{0,1:T(8,128)} fusion(bf16[2048,1536]{1,0:T(8,128)(2,1)} %all-gather.16.cloned.1.call-done, bf16[560,1536]{1,0:T(8,128)(2,1)} %all-gather.14.cloned.1.call-done), kind=kOutput, calls=%fused_computation.189 | convolution fusion | flops 3523215360 | bytes 12599296 | tf_op jit(solution)/shard_map/dot_general | solution.py:35
  330.5 53.9 %all-gather.10.cloned.1.call-done = bf16[2048,1536]{1,0:T(8,128)(2,1)} async-done(((bf16[128,1536]{1,0:T(8,128)(2,1)}), bf16[2048,1536]{1,0:T(8,128)(2,1)}) %all-gather.10.cloned.1.call-update) | async-done | bytes 6291472 | tf_op jit(solution)/shard_map/all_gather | solution.py:136
  384.4 8.9 fusion.44
  393.3 8.7 multiply_convert_fusion.2
  402.0 5.1 fusion.43
  407.2 7.6 add_convert_fusion
  416.2 8.9 convolution_convert_fusion
  425.2 73.5 %reduce-scatter.16.cloned.1.call-done = bf16[128,1536]{1,0:T(8,128)(2,1)} async-done(((bf16[2048,1536]{1,0:T(8,128)(2,1)}), bf16[128,1536]{1,0:T(8,128)(2,1)}) %reduce-scatter.16.cloned.1.call-update) | async-done | bytes 393232 | tf_op jit(solution)/shard_map/reduce_scatter | solution.py:146
  500.5 86.3 %reduce-scatter.14.cloned.1.call-done = bf16[128,1536]{1,0:T(8,128)(2,1)} async-done(((bf16[2048,1536]{1,0:T(8,128)(2,1)}), bf16[128,1536]{1,0:T(8,128)(2,1)}) %reduce-scatter.14.cloned.1.call-update) | async-done | bytes 393232 | tf_op jit(solution)/shard_map/reduce_scatter | solution.py:148
  589.1 10.8 %all_gather.39 = bf16[256,1536]{1,0:T(8,128)(2,1)S(1)} all-gather(bf16[128,1536]{1,0:T(8,128)(2,1)S(1)} %get-tuple-element.110), channel_id=1, replica_groups=mesh['dp'=4,'row'=2,'col'=4] {'row'}, dimensions={0}, use_global_device_ids=true | all-gather | bytes 1179648 | tf_op jit(solution)/shard_map/all_gather | solution.py:182
  600.8 3.4 convolution_convert_fusion.7
  606.1 5.0 fusion.38
  619.6 8.4 convolution_convert_fusion.5
  628.1 7.3 convolution_convert_fusion.4
  635.5 7.8 convolution_convert_fusion.3
  649.2 4.2 fusion.16
  660.8 5.2 reshape.593
  666.0 3.7 copy.213
  673.5 3.8 all-to-all-start.5
  678.1 2.7 convolution_convert_fusion.1
  680.9 10.1 %reduce-scatter.20.cloned.1.call-done = bf16[128,1536]{1,0:T(8,128)(2,1)} async-done(((bf16[256,1536]{1,0:T(8,128)(2,1)}), bf16[128,1536]{1,0:T(8,128)(2,1)}) %reduce-scatter.20.cloned.1.call-update) | async-done | bytes 393232 | tf_op jit(solution)/shard_map/reduce_scatter | solution.py:204
  692.3 14.5 %concatenate.92 = bf16[1536,1029]{0,1:T(8,128)(2,1)} concatenate(bf16[1536,1024]{0,1:T(8,128)(2,1)} %convolution_convert_fusion.1, bf16[1536,1]{0,1:T(2,128)(2,1)S(1)} %convert_element_type.260, bf16[1536,1]{0,1:T(2,128)(2,1)S(1)} %convert_element_type.262, bf16[1536,3]{0,1:T(4,128)(2,1)S(1)} %reshape.591), dimensions={1} | concatenate | bytes 6322176 | tf_op jit(solution)/shard_map/concatenate | solution.py:224
  706.8 5.5 copy.239
  712.3 27.7 %reduce-scatter.24.cloned.1.call-done = bf16[1,1536,560]{1,2,0:T(8,128)(2,1)} async-done(((bf16[2,1536,560]{1,2,0:T(8,128)(2,1)}), bf16[1,1536,560]{1,2,0:T(8,128)(2,1)}) %reduce-scatter.24.cloned.1.call-update) | async-done | bytes 1720336 | tf_op jit(solution)/shard_map/reduce_scatter | solution.py:159
  740.0 3.9 copy.214
  744.8 5.6 all-to-all-start.4
  754.3 53.1 %all-to-all-done.4 = bf16[16,1,96,560]{3,2,1,0:T(8,128)(2,1)S(1)} async-done(((bf16[16,1,96,560]{3,2,1,0:T(8,128)(2,1)}), bf16[16,1,96,560]{3,2,1,0:T(8,128)(2,1)S(1)}, u32[]{:S(2)}, u32[]{:S(2)}) %all-to-all-start.4) | async-done | bytes 1720352 | tf_op jit(solution)/shard_map/all_to_all | solution.py:161
  807.5 4.2 all-to-all-start.3
  813.1 3.0 copy.216
  818.7 3.0 copy.219
  829.0 3.1 copy.217
  843.1 43.4 %reduce-scatter.28.cloned.1.call-done = bf16[96,1029]{1,0:T(8,128)(2,1)} async-done(((bf16[1536,1029]{1,0:T(8,128)(2,1)}), bf16[96,1029]{1,0:T(8,128)(2,1)}) %reduce-scatter.28.cloned.1.call-update) | async-done | bytes 197584
  887.8 4.9 psum.7
  (281 shorter events, 115.4 us)
Async XLA Ops:
  7.2 11.4 %copy-start.30 = (bf16[96,4480]{1,0:T(8,128)(2,1)S(1)}, bf16[96,4480]{1,0:T(8,128)(2,1)}, u32[]{:S(2)}) copy-start(bf16[96,4480]{1,0:T(8,128)(2,1)} %param.24) | copy-start | bytes 2580484
  7.2 74.2 %all-gather.18.cloned.1.call-start = ((), (), s32[]{:S(2)}) async-start(), calls=%async_computation.28 | async-start | bytes 2506752 | tf_op jit(solution)/shard_map/all_gather | solution.py:74
  7.9 121.6 %all-gather.8.cloned.1.call-start = ((), (), s32[]{:S(2)}) async-start(), calls=%async_computation.15 | async-start | bytes 3760128 | tf_op jit(solution)/shard_map/all_gather | solution.py:59
  14.3 18.2 %all-to-all-start = ((bf16[4,128,768]{2,1,0:T(8,128)(2,1)}), bf16[4,128,768]{2,1,0:T(8,128)(2,1)}, u32[]{:S(2)}, u32[]{:S(2)}) async-start(bf16[4,128,768]{2,1,0:T(8,128)(2,1)} %bitcast), calls=%async_computation | async-start | bytes 1572864 | tf_op jit(solution)/shard_map/all_to_all | solution.py:51
  24.9 111.5 %copy-start.38 = (f32[256]{0:T(256)}, f32[256]{0:T(256)S(1)}, u32[]{:S(2)}) copy-start(f32[256]{0:T(256)S(1)} %get-tuple-element.139) | copy-start | bytes 3076
  28.1 108.3 %copy-start.44 = (f32[64]{0:T(128)}, f32[64]{0:T(128)S(1)}, u32[]{:S(2)}) copy-start(f32[64]{0:T(128)S(1)} %negate_power_fusion) | copy-start | bytes 772
  29.6 118.9 %copy-start.26 = (f32[256,64]{1,0:T(8,128)}, f32[256,64]{1,0:T(8,128)S(1)}, u32[]{:S(2)}) copy-start(f32[256,64]{1,0:T(8,128)S(1)} %get-tuple-element.131) | copy-start | bytes 196612
  32.5 127.4 %all-to-all-start.1 = ((bf16[16,1,96,560]{3,2,1,0:T(8,128)(2,1)}), bf16[16,1,96,560]{3,2,1,0:T(8,128)(2,1)}, u32[]{:S(2)}, u32[]{:S(2)}) async-start(bf16[16,1,96,560]{3,2,1,0:T(8,128)(2,1)} %bitcast.29), calls=%async_computation.2 | async-start | bytes 3932160 | tf_op jit(solution)/shard_map/all_to_all | solution.py:90
  38.3 143.1 %reduce-scatter.12.cloned.1.call-start = ((), (), s32[]{:S(2)}) async-start(), calls=%async_computation.16 | async-start | bytes 1179648 | tf_op jit(solution)/shard_map/reduce_scatter | solution.py:133
  39.8 45.1 %copy-start.7 = (bf16[4,128,768]{1,2,0:T(8,128)(2,1)}, bf16[4,128,768]{1,2,0:T(8,128)(2,1)S(1)}, u32[]{:S(2)}) copy-start(bf16[4,128,768]{1,2,0:T(8,128)(2,1)S(1)} %copy.182) | copy-start | bytes 2359300
  53.2 31.7 %copy-start.17 = (bf16[256,1536]{1,0:T(8,128)(2,1)}, bf16[256,1536]{1,0:T(8,128)(2,1)S(1)}, u32[]{:S(2)}) copy-start(bf16[256,1536]{1,0:T(8,128)(2,1)S(1)} %all_gather.30) | copy-start | bytes 2359300
  53.5 79.2 %copy-start.50 = (f32[256]{0:T(256)}, f32[256]{0:T(256)S(1)}, u32[]{:S(2)}) copy-start(f32[256]{0:T(256)S(1)} %add_rsqrt_fusion) | copy-start | bytes 3076
  85.3 72.0 %copy-start.4 = (bf16[96,8,4,384]{3,1,2,0:T(8,128)(2,1)}, bf16[96,8,4,384]{3,1,2,0:T(8,128)(2,1)S(1)}, u32[]{:S(2)}) copy-start(bf16[96,8,4,384]{3,1,2,0:T(8,128)(2,1)S(1)} %copy.247) | copy-start | bytes 7077892
  159.8 66.5 %all-gather.12.cloned.1.call-start = ((), (), s32[]{:S(2)}) async-start(), calls=%async_computation.18 | async-start | bytes 5160960 | tf_op jit(solution)/shard_map/all_gather | solution.py:92
  163.8 16.1 %copy-start.25 = (bf16[1,128,4,384]{1,3,0,2:T(8,128)(2,1)S(1)}, bf16[1,128,4,384]{1,3,0,2:T(8,128)(2,1)}, u32[]{:S(2)}) copy-start(bf16[1,128,4,384]{1,3,0,2:T(8,128)(2,1)} %get-tuple-element.111) | copy-start | bytes 1179652
  163.9 93.4 %all-gather.14.cloned.1.call-start = ((), (), s32[]{:S(2)}) async-start(), calls=%async_computation.19 | async-start | bytes 2580480 | tf_op jit(solution)/shard_map/all_gather | solution.py:97
  179.9 141.5 %all-gather.16.cloned.1.call-start = ((), (), s32[]{:S(2)}) async-start(), calls=%async_computation.21 | async-start | bytes 6684672 | tf_op jit(solution)/shard_map/all_gather | solution.py:98
  180.9 203.5 %all-gather.10.cloned.1.call-start = ((), (), s32[]{:S(2)}) async-start(), calls=%async_computation.17 | async-start | bytes 6684672 | tf_op jit(solution)/shard_map/all_gather | solution.py:136
  185.6 313.0 %reduce-scatter.16.cloned.1.call-start = ((), (), s32[]{:S(2)}) async-start(), calls=%async_computation.22 | async-start | bytes 6684672 | tf_op jit(solution)/shard_map/reduce_scatter | solution.py:146
  384.4 9.0 copy-start.52
  384.4 9.0 copy-start.57
  393.3 8.7 copy-start.29
  414.7 172.1 %reduce-scatter.14.cloned.1.call-start = ((), (), s32[]{:S(2)}) async-start(), calls=%async_computation.20 | async-start | bytes 6684672 | tf_op jit(solution)/shard_map/reduce_scatter | solution.py:148
  425.1 73.5 %copy-start.3 = (bf16[128,1536]{1,0:T(8,128)(2,1)S(1)}, bf16[128,1536]{1,0:T(8,128)(2,1)}, u32[]{:S(2)}) copy-start(bf16[128,1536]{1,0:T(8,128)(2,1)} %reduce-scatter.12.cloned.1.call-done) | copy-start | bytes 1179652
  425.1 73.5 %copy-start.42 = (f32[128]{0:T(128)S(1)}, f32[128]{0:T(128)}, u32[]{:S(2)}) copy-start(f32[128]{0:T(128)} %copy-done.41) | copy-start | bytes 1540
  425.1 161.7 %copy-start.6 = (bf16[128,1536]{1,0:T(8,128)(2,1)S(1)}, bf16[128,1536]{1,0:T(8,128)(2,1)}, u32[]{:S(2)}) copy-start(bf16[128,1536]{1,0:T(8,128)(2,1)} %copy.237) | copy-start | bytes 1179652
  425.1 161.7 %copy-start.48 = (f32[128]{0:T(128)S(1)}, f32[128]{0:T(128)}, u32[]{:S(2)}) copy-start(f32[128]{0:T(128)} %get-tuple-element.136) | copy-start | bytes 1540
  425.1 222.8 %reduce-scatter.18.cloned.1.call-start = ((), (), s32[]{:S(2)}) async-start(), calls=%async_computation.23 | async-start | bytes 655360 | tf_op jit(solution)/shard_map/reduce_scatter | solution.py:198
  500.5 88.5 %copy-start.46 = (f32[128]{0:T(128)}, f32[128]{0:T(128)S(1)}, u32[]{:S(2)}) copy-start(f32[128]{0:T(128)S(1)} %get-tuple-element.87) | copy-start | bytes 1540
  600.8 10.3 %slice-start = ((s8[6291456]{0:T(1024)(128)(4,1)}), s8[2097152]{0:T(1024)(128)(4,1)S(1)}, s32[]{:S(2)}) async-start(s8[6291456]{0:T(1024)(128)(4,1)} %bitcast.261), calls=%async_computation.30 | async-start | bytes 4194304
  619.3 52.0 %reduce-scatter.26.cloned.1.call-start = ((), (), s32[]{:S(2)}) async-start(), calls=%async_computation.27 | async-start | bytes 2580480 | tf_op jit(solution)/shard_map/reduce_scatter | solution.py:162
  628.0 63.0 %reduce-scatter.20.cloned.1.call-start = ((), (), s32[]{:S(2)}) async-start(), calls=%async_computation.24 | async-start | bytes 1179648 | tf_op jit(solution)/shard_map/reduce_scatter | solution.py:204
  635.4 7.8 copy-start.2
  635.4 7.8 copy-start.21
  653.4 86.6 %reduce-scatter.24.cloned.1.call-start = ((), (), s32[]{:S(2)}) async-start(), calls=%async_computation.26 | async-start | bytes 5160960 | tf_op jit(solution)/shard_map/reduce_scatter | solution.py:159
  657.4 184.0 %reduce-scatter.22.cloned.1.call-start = ((), (), s32[]{:S(2)}) async-start(), calls=%async_computation.25 | async-start | bytes 2506752 | tf_op jit(solution)/shard_map/reduce_scatter | solution.py:185
  669.7 7.6 copy-start.24
  669.7 8.4 copy-start.18
  669.7 8.4 copy-start.35
  669.7 8.4 copy-start.51
  673.5 70.4 %all-to-all-start.5 = ((bf16[4,280,384]{2,1,0:T(8,128)(2,1)}), bf16[4,280,384]{2,1,0:T(8,128)(2,1)S(1)}, u32[]{:S(2)}, u32[]{:S(2)}) async-start(bf16[4,280,384]{2,1,0:T(8,128)(2,1)} %bitcast.259), calls=%async_computation.13 | async-start | bytes 1720320 | tf_op jit(solution)/shard_map/all_to_all | solution.py:164
  677.2 209.2 %reduce-scatter.28.cloned.1.call-start = ((), (), s32[]{:S(2)}) async-start(), calls=%async_computation.29 | async-start | bytes 3760128
  712.3 38.1 %copy-start.43 = (f32[128]{0:T(128)S(1)}, f32[128]{0:T(128)}, u32[]{:S(2)}) copy-start(f32[128]{0:T(128)} %copy-done.41) | copy-start | bytes 1540
  712.3 38.1 %copy-start.47 = (f32[128]{0:T(128)S(1)}, f32[128]{0:T(128)}, u32[]{:S(2)}) copy-start(f32[128]{0:T(128)} %copy-done.46) | copy-start | bytes 1540
  712.3 38.1 %copy-start.49 = (f32[128]{0:T(128)S(1)}, f32[128]{0:T(128)}, u32[]{:S(2)}) copy-start(f32[128]{0:T(128)} %get-tuple-element.136) | copy-start | bytes 1540
  744.8 62.7 %all-to-all-start.4 = ((bf16[16,1,96,560]{3,2,1,0:T(8,128)(2,1)}), bf16[16,1,96,560]{3,2,1,0:T(8,128)(2,1)S(1)}, u32[]{:S(2)}, u32[]{:S(2)}) async-start(bf16[16,1,96,560]{3,2,1,0:T(8,128)(2,1)} %bitcast.78), calls=%async_computation.11 | async-start | bytes 3932160 | tf_op jit(solution)/shard_map/all_to_all | solution.py:161
  752.2 59.5 %copy-start.14 = (bf16[4,280,384]{2,1,0:T(8,128)(2,1)S(1)}, bf16[4,280,384]{2,1,0:T(8,128)(2,1)}, u32[]{:S(2)}) copy-start(bf16[4,280,384]{2,1,0:T(8,128)(2,1)} %copy-done.13) | copy-start | bytes 2580484
  807.5 31.9 %all-to-all-start.3 = ((bf16[4,128,768]{2,1,0:T(8,128)(2,1)}), bf16[4,128,768]{2,1,0:T(8,128)(2,1)}, u32[]{:S(2)}, u32[]{:S(2)}) async-start(bf16[4,128,768]{2,1,0:T(8,128)(2,1)} %maximum_bitcast_fusion.2), calls=%async_computation.8 | async-start | bytes 1572864 | tf_op jit(solution)/shard_map/all_to_all | solution.py:231
  (32 other events, 103.0 us)
Sparse Core Ops, SparseCore 0:
  10.3 71.0 all-gather.17
  84.3 45.1 all-gather.7
  160.0 16.1 reduce-scatter.11
  178.1 48.2 all-gather.11
  228.3 28.8 all-gather.13
  259.9 61.3 all-gather.15
  324.2 60.0 all-gather.9
  414.9 83.7 reduce-scatter.15
  502.6 84.1 reduce-scatter.13
  619.5 21.1 reduce-scatter.17
  643.5 27.7 reduce-scatter.25
  673.4 17.5 reduce-scatter.19
  693.2 46.6 reduce-scatter.23
  743.6 71.7 reduce-scatter.21
  819.1 67.3 reduce-scatter.27
